TPU v7x, 256 devices: a whole 4x4x8 slice. The times are simulated.
256 devices in a mesh: ep: 8 (over z), tp: 32 (over y, x, core).
Axes of the slice: x: 4, y: 4, z: 8, core: 2. Of those that a mesh axis runs over, the one named last changes fastest.
Arguments:
- tokens: bfloat16 [768, 3072], P('ep', 'tp'), may hold values from -6 to 6
- cotangent: bfloat16 [768, 3072], P('ep', 'tp'), may hold values from -6 to 6
- expert_ids: int32 [768, 2], P('ep'), may hold values from 0 to 7, all different within a row; in each aligned block of 96 rows (0 to 95, 96 to 191, ...) at most 40 rows name the same one
- combine_weights: float32 [768, 2], P('ep'), may hold values from 0.1 to 1
- w_gate: bfloat16 [8, 3072, 8192], P('ep', None, 'tp'), may hold values from -0.21875 to 0.21875
- w_up: bfloat16 [8, 3072, 8192], P('ep', None, 'tp'), may hold values from -0.109375 to 0.109375
- w_down: bfloat16 [8, 8192, 3072], P('ep', 'tp'), may hold values from -0.125 to 0.125
Outputs:
- mixed: bfloat16 [768, 3072], P('ep', 'tp')
- grad_tokens: bfloat16 [768, 3072], P('ep', 'tp')
- grad_combine: float32 [768, 2], P('ep')
- grad_gate: bfloat16 [8, 3072, 8192], P('ep', 'tp')
- grad_up: bfloat16 [8, 3072, 8192], P('ep', 'tp')
- grad_down: bfloat16 [8, 8192, 3072], P('ep', None, 'tp')
Inputs may be any that keep to these rules, and one draw needn't show every extreme that they name: `expert_ids`: each row names 2 different experts. Among the 96 rows of one index of ep, no expert is named more than 40 times, and in some such blocks one expert is named exactly 40 times.
All inputs are finite; a program needn't handle non-finite values.
Results may differ from a plain program's by a relative error of at most 0.019.
Values may be sent and summed in bfloat16 or wider, within the bound.
No kernel may reach another device: no remote copies, remote signals or barrier semaphores. Data moves between devices by JAX's collectives and lax.ppermute only.
A program may use at most 64 MiB of HBM per device.

v0:
```python
import jax
import jax.numpy as jnp
from jax import lax
from jax.sharding import PartitionSpec as P


def in_one_piece(arrays, axis, split_dim, concat_dim, along):
    ends, at = ([], 0)
    for a in arrays[:-1]:
        at += a.shape[along]
        ends.append(at)
    both = jnp.concatenate(arrays, axis=along)
    return tuple(
        jnp.split(
            lax.all_to_all(both, axis, split_axis=split_dim, concat_axis=concat_dim, tiled=True),
            ends,
            axis=along,
        )
    )


def laid_out(pieces, dim):
    pieces = jnp.moveaxis(pieces, 0, dim)
    lengths = pieces.shape
    return pieces.reshape(*lengths[:dim], lengths[dim] * lengths[dim + 1], *lengths[dim + 2 :])


def copy_for_each(x, axis):
    devices = lax.axis_size(axis)
    return lax.all_to_all(jnp.broadcast_to(x[None], (devices, *x.shape)), axis, 0, 0, tiled=True)


def collect(x, axis, dim):
    return laid_out(copy_for_each(x, axis), dim)


def split_up(x, dim, devices):
    lengths = x.shape
    pieces = x.reshape(*lengths[:dim], devices, lengths[dim] // devices, *lengths[dim + 1 :])
    return jnp.moveaxis(pieces, dim, 0)


def sum_at_owner(x, axis, dim):
    devices = lax.axis_size(axis)
    pieces = lax.all_to_all(split_up(x, dim, devices), axis, 0, 0, tiled=True)
    return jnp.sum(pieces.astype(jnp.float32), axis=0)


def over_copies(x, axis):
    return copy_for_each(x, axis).sum(axis=0)


def silu_parts(gate_pre):
    sigma = jax.nn.sigmoid(gate_pre)
    return (gate_pre * sigma, sigma * (1.0 + gate_pre * (1.0 - sigma)))


def contract_rows(left, right):
    return lax.dot_general(
        left, right, (((0,), (0,)), ((), ())), preferred_element_type=jnp.float32
    )


def contract_cols(left, right):
    return lax.dot_general(
        left, right, (((1,), (1,)), ((), ())), preferred_element_type=jnp.float32
    )


def body(tokens, cotangent, expert_ids, combine_weights, w_gate, w_up, w_down):
    groups = lax.axis_size("ep")
    tok_rows, piece_width = tokens.shape
    chosen = expert_ids.shape[1]
    capacity = tok_rows * chosen * 5 // (3 * groups)
    buffer_rows = groups * capacity
    gate_weight = w_gate[0]
    up_weight = w_up[0]
    down_weight = w_down[0]
    hidden_width = gate_weight.shape[1]
    flat_ids = expert_ids.reshape(-1)
    onehot = (flat_ids[:, None] == jnp.arange(groups, dtype=jnp.int32)[None, :]).astype(jnp.int32)
    rank = jnp.sum((jnp.cumsum(onehot, axis=0) - onehot) * onehot, axis=1)
    slot_index = flat_ids * capacity + rank
    places = (jnp.arange(buffer_rows, dtype=jnp.int32)[:, None] == slot_index[None, :]).astype(
        jnp.bfloat16
    )
    placer = jnp.sum(
        places.reshape(buffer_rows, tok_rows, chosen).astype(jnp.float32), axis=2
    ).astype(jnp.bfloat16)
    scaled = (combine_weights[:, :, None] * cotangent[:, None, :].astype(jnp.float32)).astype(
        jnp.bfloat16
    )
    send_grad = jnp.dot(
        places, scaled.reshape(tok_rows * chosen, piece_width), preferred_element_type=jnp.float32
    ).astype(jnp.bfloat16)
    send_rows = jnp.dot(placer, tokens, preferred_element_type=jnp.float32).astype(jnp.bfloat16)
    recv_rows, recv_grad = in_one_piece(
        (
            send_rows.reshape(groups, capacity, piece_width),
            send_grad.reshape(groups, capacity, piece_width),
        ),
        "ep",
        0,
        0,
        1,
    )
    recv_rows = recv_rows.reshape(buffer_rows, piece_width)
    piece = collect(recv_rows, "tp", 1)
    gate_pre = jnp.dot(piece, gate_weight, preferred_element_type=jnp.float32)
    up_pre = jnp.dot(piece, up_weight, preferred_element_type=jnp.float32)
    recv_grad = recv_grad.reshape(buffer_rows, piece_width)
    active, slope = silu_parts(gate_pre)
    hidden = (active * up_pre).astype(jnp.bfloat16)
    partial_value = jnp.dot(hidden, down_weight, preferred_element_type=jnp.float32)
    out_piece = sum_at_owner(partial_value.astype(jnp.bfloat16), "tp", 1).astype(jnp.bfloat16)
    out_back = lax.all_to_all(
        out_piece.reshape(groups, capacity, piece_width),
        "ep",
        split_axis=0,
        concat_axis=0,
        tiled=True,
    ).reshape(buffer_rows, piece_width)
    out_tokens = (
        jnp.take(out_back, slot_index, axis=0)
        .reshape(tok_rows, chosen, piece_width)
        .astype(jnp.float32)
    )
    mixed = jnp.sum(combine_weights[:, :, None] * out_tokens, axis=1).astype(jnp.bfloat16)
    local_products = jnp.sum(cotangent.astype(jnp.float32)[:, None, :] * out_tokens, axis=2)
    grad_combine = over_copies(local_products, "tp")
    grad_hidden = contract_cols(collect(recv_grad, "tp", 1), down_weight)
    down_grad = contract_rows(hidden, collect(recv_grad, "tp", 1))
    grad_gate_pre = (grad_hidden * up_pre * slope).astype(jnp.bfloat16)
    grad_up_pre = (grad_hidden * active).astype(jnp.bfloat16)
    input_partial = contract_cols(grad_gate_pre, gate_weight) + contract_cols(
        grad_up_pre, up_weight
    )
    input_piece = sum_at_owner(input_partial.astype(jnp.bfloat16), "tp", 1).astype(jnp.bfloat16)
    input_back = lax.all_to_all(
        input_piece.reshape(groups, capacity, piece_width),
        "ep",
        split_axis=0,
        concat_axis=0,
        tiled=True,
    ).reshape(buffer_rows, piece_width)
    grad_tokens = jnp.sum(
        jnp.take(input_back, slot_index, axis=0)
        .reshape(tok_rows, chosen, piece_width)
        .astype(jnp.float32),
        axis=1,
    ).astype(jnp.bfloat16)
    stacked = jnp.concatenate([grad_gate_pre, grad_up_pre], axis=1)
    both_grads = contract_rows(collect(recv_rows, "tp", 1), stacked)
    gate_grad = both_grads[:, :hidden_width].astype(jnp.bfloat16)
    up_grad = both_grads[:, hidden_width:].astype(jnp.bfloat16)
    gate_rows_out, up_rows_out = (
        lax.all_to_all(gate_grad, "tp", split_axis=0, concat_axis=1, tiled=True),
        lax.all_to_all(up_grad, "tp", split_axis=0, concat_axis=1, tiled=True),
    )
    down_cols_out = lax.all_to_all(
        down_grad.astype(jnp.bfloat16), "tp", split_axis=1, concat_axis=0, tiled=True
    )
    return (
        mixed,
        grad_tokens,
        grad_combine,
        gate_rows_out[None],
        up_rows_out[None],
        down_cols_out[None],
    )


def solution(mesh):
    placed = (
        P("ep", "tp"),
        P("ep", "tp"),
        P("ep", None),
        P("ep", None),
        P("ep", None, "tp"),
        P("ep", None, "tp"),
        P("ep", "tp", None),
    )
    return jax.shard_map(
        body,
        mesh=mesh,
        in_specs=placed,
        out_specs=(
            P("ep", "tp"),
            P("ep", "tp"),
            P("ep", None),
            P("ep", "tp", None),
            P("ep", "tp", None),
            P("ep", None, "tp"),
        ),
        check_vma=False,
    )
```

profile of v0, /device:TPU:1, one launch (start us, length us, event | category | flops | bytes accessed | tf_op | source)
XLA Modules:
  0.0 327.7 jit_solution(8326589695224463317)
XLA Ops:
  7.6 17.0 %all_to_all.90 = bf16[8,80,96]{2,1,0:T(8,128)(2,1)S(1)} all-to-all(bf16[8,80,96]{2,1,0:T(8,128)(2,1)S(1)} %pad_maximum_fusion), channel_id=1, replica_groups=mesh['ep'=8,'tp'=32] {'ep'}, dimensions={0} | all-to-all | bytes 245760 | tf_op jit(solution)/shard_map/all_to_all | solution.py:15
  26.3 9.6 %all-to-all-start.1 = ((bf16[32,320,96]{1,2,0:T(8,128)(2,1)}), bf16[32,320,96]{1,2,0:T(8,128)(2,1)}, u32[]{:S(2)}, u32[]{:S(2)}) async-start(bf16[32,320,96]{1,2,0:T(8,128)(2,1)} %broadcast_in_dim.28), calls=%async_computation.1 | async-start | bytes 4718592 | tf_op jit(solution)/shard_map/all_to_all | solution.py:30
  36.1 31.4 %all-to-all-done.1 = bf16[32,320,96]{1,2,0:T(8,128)(2,1)} async-done(((bf16[32,320,96]{1,2,0:T(8,128)(2,1)}), bf16[32,320,96]{1,2,0:T(8,128)(2,1)}, u32[]{:S(2)}, u32[]{:S(2)}) %all-to-all-start.1) | async-done | bytes 1966112 | tf_op jit(solution)/shard_map/all_to_all | solution.py:30
  69.2 6.4 %all-to-all-start.4 = ((bf16[32,320,96]{1,2,0:T(8,128)(2,1)}), bf16[32,320,96]{1,2,0:T(8,128)(2,1)}, u32[]{:S(2)}, u32[]{:S(2)}) async-start(bf16[32,320,96]{1,2,0:T(8,128)(2,1)} %broadcast_in_dim.30), calls=%async_computation.4 | async-start | bytes 4718592 | tf_op jit(solution)/shard_map/all_to_all | solution.py:30
  80.7 26.2 %all-to-all-done.4 = bf16[32,320,96]{1,2,0:T(8,128)(2,1)} async-done(((bf16[32,320,96]{1,2,0:T(8,128)(2,1)}), bf16[32,320,96]{1,2,0:T(8,128)(2,1)}, u32[]{:S(2)}, u32[]{:S(2)}) %all-to-all-start.4) | async-done | bytes 1966112 | tf_op jit(solution)/shard_map/all_to_all | solution.py:30
  106.9 3.4 %multiply_convert_fusion = (bf16[320,256]{1,0:T(8,128)(2,1)}, bf16[320,256]{1,0:T(8,128)(2,1)}, bf16[320,256]{1,0:T(8,128)(2,1)S(1)}) fusion(f32[320,256]{1,0:T(8,128)S(1)} %fusion.9, f32[320,256]{1,0:T(8,128)S(1)} %fusion.5, bf16[320,3072]{0,1:T(8,128)(2,1)} %bitcast.20, bf16[1,256,3072]{2,1,0:T(8,128)(2,1)S(1)} %copy-done), kind=kOutput, calls=%fused_computation.22 | convolution fusion | flops 504545280 | bytes 4685824 | tf_op jit(solution)/shard_map/dot_general | solution.py:65
  110.9 2.7 convolution_convert_fusion.2
  115.2 6.0 %all-to-all-start.10 = ((bf16[256,32,96]{0,2,1:T(8,128)(2,1)}), bf16[256,32,96]{0,2,1:T(8,128)(2,1)S(1)}, u32[]{:S(2)}, u32[]{:S(2)}) async-start(bf16[256,32,96]{0,2,1:T(8,128)(2,1)} %bitcast.69), calls=%async_computation.10 | async-start | bytes 3145728 | tf_op jit(solution)/shard_map/all_to_all | solution.py:160
  121.3 3.5 %convolution_convert_fusion = bf16[3072,512]{1,0:T(8,128)(2,1)S(1)} fusion(bf16[320,3072]{0,1:T(8,128)(2,1)} %bitcast.8, bf16[320,256]{1,0:T(8,128)(2,1)S(1)} %copy-done.15, bf16[320,256]{1,0:T(8,128)(2,1)S(1)} %copy-done.13), kind=kOutput, calls=%fused_computation.2 | convolution fusion | flops 1008861184 | bytes 5439488 | tf_op jit(solution)/shard_map/dot_general | solution.py:59
  126.6 17.0 %all-to-all-done.10 = bf16[256,32,96]{0,2,1:T(8,128)(2,1)S(1)} async-done(((bf16[256,32,96]{0,2,1:T(8,128)(2,1)}), bf16[256,32,96]{0,2,1:T(8,128)(2,1)S(1)}, u32[]{:S(2)}, u32[]{:S(2)}) %all-to-all-start.10) | async-done | bytes 1572896 | tf_op jit(solution)/shard_map/all_to_all | solution.py:160
  143.6 29.0 %all_to_all.91 = bf16[32,96,256]{2,1,0:T(8,128)(2,1)} all-to-all(bf16[32,96,256]{2,1,0:T(8,128)(2,1)} %bitcast.71), channel_id=1, replica_groups=mesh['ep'=8,'tp'=32] {'tp'}, dimensions={0} | all-to-all | bytes 3145728 | tf_op jit(solution)/shard_map/all_to_all | solution.py:157
  172.7 4.7 %all-to-all-start.9 = ((bf16[32,96,256]{2,1,0:T(8,128)(2,1)}), bf16[32,96,256]{2,1,0:T(8,128)(2,1)}, u32[]{:S(2)}, u32[]{:S(2)}) async-start(bf16[32,96,256]{2,1,0:T(8,128)(2,1)} %bitcast.70), calls=%async_computation.9 | async-start | bytes 3145728 | tf_op jit(solution)/shard_map/all_to_all | solution.py:158
  181.4 18.3 %all-to-all-done.9 = bf16[32,96,256]{2,1,0:T(8,128)(2,1)} async-done(((bf16[32,96,256]{2,1,0:T(8,128)(2,1)}), bf16[32,96,256]{2,1,0:T(8,128)(2,1)}, u32[]{:S(2)}, u32[]{:S(2)}) %all-to-all-start.9) | async-done | bytes 1572896 | tf_op jit(solution)/shard_map/all_to_all | solution.py:158
  199.7 6.4 %all-to-all-start.2 = ((bf16[32,320,96]{1,2,0:T(8,128)(2,1)}), bf16[32,320,96]{1,2,0:T(8,128)(2,1)}, u32[]{:S(2)}, u32[]{:S(2)}) async-start(bf16[32,320,96]{1,2,0:T(8,128)(2,1)} %bitcast.65), calls=%async_computation.2 | async-start | bytes 4718592 | tf_op jit(solution)/shard_map/all_to_all | solution.py:45
  210.8 26.6 %all-to-all-done.2 = bf16[32,320,96]{1,2,0:T(8,128)(2,1)} async-done(((bf16[32,320,96]{1,2,0:T(8,128)(2,1)}), bf16[32,320,96]{1,2,0:T(8,128)(2,1)}, u32[]{:S(2)}, u32[]{:S(2)}) %all-to-all-start.2) | async-done | bytes 1966112 | tf_op jit(solution)/shard_map/all_to_all | solution.py:45
  237.4 6.8 %all-to-all-start.5 = ((bf16[32,320,96]{1,2,0:T(8,128)(2,1)}), bf16[32,320,96]{1,2,0:T(8,128)(2,1)}, u32[]{:S(2)}, u32[]{:S(2)}) async-start(bf16[32,320,96]{1,2,0:T(8,128)(2,1)} %bitcast.66), calls=%async_computation.5 | async-start | bytes 4718592 | tf_op jit(solution)/shard_map/all_to_all | solution.py:45
  247.1 28.4 %all-to-all-done.5 = bf16[32,320,96]{1,2,0:T(8,128)(2,1)} async-done(((bf16[32,320,96]{1,2,0:T(8,128)(2,1)}), bf16[32,320,96]{1,2,0:T(8,128)(2,1)}, u32[]{:S(2)}, u32[]{:S(2)}) %all-to-all-start.5) | async-done | bytes 1966112 | tf_op jit(solution)/shard_map/all_to_all | solution.py:45
  275.4 3.4 %all-to-all-start.3 = ((bf16[8,40,96]{2,1,0:T(8,128)(2,1)}), bf16[8,40,96]{2,1,0:T(8,128)(2,1)S(1)}, u32[]{:S(2)}, u32[]{:S(2)}) async-start(bf16[8,40,96]{2,1,0:T(8,128)(2,1)} %bitcast.15), calls=%async_computation.3 | async-start | bytes 163840 | tf_op jit(solution)/shard_map/all_to_all | solution.py:116
  280.9 3.9 %broadcast_in_dim.61 = bf16[1,8192,96]{1,2,0:T(8,128)(2,1)} reshape(bf16[32,256,96]{1,0,2:T(8,128)(2,1)} %copy.120) | data formatting | bytes 3145728 | tf_op jit(solution)/shard_map/broadcast_in_dim | solution.py:169
  286.7 3.7 %broadcast_in_dim.59 = bf16[1,96,8192]{2,1,0:T(8,128)(2,1)} reshape(bf16[96,32,256]{2,1,0:T(8,128)(2,1)} %copy.117) | data formatting | bytes 3145728 | tf_op jit(solution)/shard_map/broadcast_in_dim | solution.py:167
  297.7 6.6 %all-to-all-start.6 = ((bf16[8,40,96]{2,1,0:T(8,128)(2,1)}), bf16[8,40,96]{2,1,0:T(8,128)(2,1)S(1)}, u32[]{:S(2)}, u32[]{:S(2)}) async-start(bf16[8,40,96]{2,1,0:T(8,128)(2,1)} %bitcast.23), calls=%async_computation.6 | async-start | bytes 163840 | tf_op jit(solution)/shard_map/all_to_all | solution.py:139
  305.4 6.3 %all-to-all-done.6 = bf16[8,40,96]{2,1,0:T(8,128)(2,1)S(1)} async-done(((bf16[8,40,96]{2,1,0:T(8,128)(2,1)}), bf16[8,40,96]{2,1,0:T(8,128)(2,1)S(1)}, u32[]{:S(2)}, u32[]{:S(2)}) %all-to-all-start.6) | async-done | bytes 61472 | tf_op jit(solution)/shard_map/all_to_all | solution.py:139
  312.4 7.4 %all-to-all-start.7 = ((f32[32,96,2]{1,2,0:T(2,128)}), f32[32,96,2]{1,2,0:T(2,128)S(1)}, u32[]{:S(2)}, u32[]{:S(2)}) async-start(f32[32,96,2]{1,2,0:T(2,128)} %broadcast_in_dim.58), calls=%async_computation.7 | async-start | bytes 65536 | tf_op jit(solution)/shard_map/all_to_all | solution.py:30
  322.2 4.9 %all-to-all-done.7 = f32[32,96,2]{1,2,0:T(2,128)S(1)} async-done(((f32[32,96,2]{1,2,0:T(2,128)}), f32[32,96,2]{1,2,0:T(2,128)S(1)}, u32[]{:S(2)}, u32[]{:S(2)}) %all-to-all-start.7) | async-done | bytes 24608 | tf_op jit(solution)/shard_map/all_to_all | solution.py:30
  (92 shorter events, 47.1 us)
Async XLA Ops:
  0.6 106.3 %copy-start = (bf16[1,256,3072]{2,1,0:T(8,128)(2,1)S(1)}, bf16[1,256,3072]{2,1,0:T(8,128)(2,1)}, u32[]{:S(2)}) copy-start(bf16[1,256,3072]{2,1,0:T(8,128)(2,1)} %param.15) | copy-start | bytes 4718596
  3.6 22.7 %copy-start.11 = (f32[96,2]{1,0:T(8,128)}, f32[96,2]{1,0:T(8,128)S(1)}, u32[]{:S(2)}) copy-start(f32[96,2]{1,0:T(8,128)S(1)} %copy.104) | copy-start | bytes 2308
  26.3 41.2 %all-to-all-start.1 = ((bf16[32,320,96]{1,2,0:T(8,128)(2,1)}), bf16[32,320,96]{1,2,0:T(8,128)(2,1)}, u32[]{:S(2)}, u32[]{:S(2)}) async-start(bf16[32,320,96]{1,2,0:T(8,128)(2,1)} %broadcast_in_dim.28), calls=%async_computation.1 | async-start | bytes 4718592 | tf_op jit(solution)/shard_map/all_to_all | solution.py:30
  69.2 6.4 %copy-start.6 = (bf16[1,3072,256]{2,1,0:T(8,128)(2,1)S(1)}, bf16[1,3072,256]{2,1,0:T(8,128)(2,1)}, u32[]{:S(2)}) copy-start(bf16[1,3072,256]{2,1,0:T(8,128)(2,1)} %param.14) | copy-start | bytes 4718596
  69.2 37.7 %all-to-all-start.4 = ((bf16[32,320,96]{1,2,0:T(8,128)(2,1)}), bf16[32,320,96]{1,2,0:T(8,128)(2,1)}, u32[]{:S(2)}, u32[]{:S(2)}) async-start(bf16[32,320,96]{1,2,0:T(8,128)(2,1)} %broadcast_in_dim.30), calls=%async_computation.4 | async-start | bytes 4718592 | tf_op jit(solution)/shard_map/all_to_all | solution.py:30
  75.6 2.6 copy-start.4
  115.2 6.1 %copy-start.13 = (bf16[320,256]{1,0:T(8,128)(2,1)S(1)}, bf16[320,256]{1,0:T(8,128)(2,1)}, u32[]{:S(2)}) copy-start(bf16[320,256]{1,0:T(8,128)(2,1)} %get-tuple-element.12) | copy-start | bytes 491524
  115.2 6.1 %copy-start.15 = (bf16[320,256]{1,0:T(8,128)(2,1)S(1)}, bf16[320,256]{1,0:T(8,128)(2,1)}, u32[]{:S(2)}) copy-start(bf16[320,256]{1,0:T(8,128)(2,1)} %get-tuple-element.11) | copy-start | bytes 491524
  115.2 28.4 %all-to-all-start.10 = ((bf16[256,32,96]{0,2,1:T(8,128)(2,1)}), bf16[256,32,96]{0,2,1:T(8,128)(2,1)S(1)}, u32[]{:S(2)}, u32[]{:S(2)}) async-start(bf16[256,32,96]{0,2,1:T(8,128)(2,1)} %bitcast.69), calls=%async_computation.10 | async-start | bytes 3145728 | tf_op jit(solution)/shard_map/all_to_all | solution.py:160
  143.6 29.0 %copy-start.1 = (bf16[256,32,96]{0,2,1:T(8,128)(2,1)}, bf16[256,32,96]{0,2,1:T(8,128)(2,1)S(1)}, u32[]{:S(2)}) copy-start(bf16[256,32,96]{0,2,1:T(8,128)(2,1)S(1)} %all-to-all-done.10) | copy-start | bytes 4718596
  172.7 27.1 %all-to-all-start.9 = ((bf16[32,96,256]{2,1,0:T(8,128)(2,1)}), bf16[32,96,256]{2,1,0:T(8,128)(2,1)}, u32[]{:S(2)}, u32[]{:S(2)}) async-start(bf16[32,96,256]{2,1,0:T(8,128)(2,1)} %bitcast.70), calls=%async_computation.9 | async-start | bytes 3145728 | tf_op jit(solution)/shard_map/all_to_all | solution.py:158
  199.7 6.5 %copy-start.5 = (bf16[1,3072,256]{2,1,0:T(8,128)(2,1)S(1)}, bf16[1,3072,256]{2,1,0:T(8,128)(2,1)}, u32[]{:S(2)}) copy-start(bf16[1,3072,256]{2,1,0:T(8,128)(2,1)} %param.13) | copy-start | bytes 4718596
  199.7 6.5 %copy-start.14 = (bf16[320,256]{1,0:T(8,128)(2,1)S(1)}, bf16[320,256]{1,0:T(8,128)(2,1)}, u32[]{:S(2)}) copy-start(bf16[320,256]{1,0:T(8,128)(2,1)} %get-tuple-element.12) | copy-start | bytes 491524
  199.7 37.6 %all-to-all-start.2 = ((bf16[32,320,96]{1,2,0:T(8,128)(2,1)}), bf16[32,320,96]{1,2,0:T(8,128)(2,1)}, u32[]{:S(2)}, u32[]{:S(2)}) async-start(bf16[32,320,96]{1,2,0:T(8,128)(2,1)} %bitcast.65), calls=%async_computation.2 | async-start | bytes 4718592 | tf_op jit(solution)/shard_map/all_to_all | solution.py:45
  206.2 1.4 copy-start.7
  206.2 1.4 copy-start.16
  237.4 38.1 %all-to-all-start.5 = ((bf16[32,320,96]{1,2,0:T(8,128)(2,1)}), bf16[32,320,96]{1,2,0:T(8,128)(2,1)}, u32[]{:S(2)}, u32[]{:S(2)}) async-start(bf16[32,320,96]{1,2,0:T(8,128)(2,1)} %bitcast.66), calls=%async_computation.5 | async-start | bytes 4718592 | tf_op jit(solution)/shard_map/all_to_all | solution.py:45
  244.2 34.7 %copy-start.2 = (bf16[256,32,96]{0,2,1:T(8,128)(2,1)S(1)}, bf16[256,32,96]{0,2,1:T(8,128)(2,1)}, u32[]{:S(2)}) copy-start(bf16[256,32,96]{0,2,1:T(8,128)(2,1)} %copy-done.1) | copy-start | bytes 4718596
  275.4 22.2 %all-to-all-start.3 = ((bf16[8,40,96]{2,1,0:T(8,128)(2,1)}), bf16[8,40,96]{2,1,0:T(8,128)(2,1)S(1)}, u32[]{:S(2)}, u32[]{:S(2)}) async-start(bf16[8,40,96]{2,1,0:T(8,128)(2,1)} %bitcast.15), calls=%async_computation.3 | async-start | bytes 163840 | tf_op jit(solution)/shard_map/all_to_all | solution.py:116
  280.9 3.9 %copy-start.3 = (bf16[32,96,256]{2,1,0:T(8,128)(2,1)S(1)}, bf16[32,96,256]{2,1,0:T(8,128)(2,1)}, u32[]{:S(2)}) copy-start(bf16[32,96,256]{2,1,0:T(8,128)(2,1)} %all_to_all.91) | copy-start | bytes 4718596
  294.9 10.2 %copy-start.10 = (f32[96,2,96]{2,1,0:T(2,128)S(1)}, f32[96,2,96]{2,1,0:T(2,128)}, u32[]{:S(2)}) copy-start(f32[96,2,96]{2,1,0:T(2,128)} %copy-done.9) | copy-start | bytes 221188
  294.9 25.8 %copy-start.12 = (f32[96,2]{1,0:T(8,128)S(1)}, f32[96,2]{1,0:T(8,128)}, u32[]{:S(2)}) copy-start(f32[96,2]{1,0:T(8,128)} %copy-done.11) | copy-start | bytes 2308
  297.7 14.1 %all-to-all-start.6 = ((bf16[8,40,96]{2,1,0:T(8,128)(2,1)}), bf16[8,40,96]{2,1,0:T(8,128)(2,1)S(1)}, u32[]{:S(2)}, u32[]{:S(2)}) async-start(bf16[8,40,96]{2,1,0:T(8,128)(2,1)} %bitcast.23), calls=%async_computation.6 | async-start | bytes 163840 | tf_op jit(solution)/shard_map/all_to_all | solution.py:139
  312.4 14.7 %all-to-all-start.7 = ((f32[32,96,2]{1,2,0:T(2,128)}), f32[32,96,2]{1,2,0:T(2,128)S(1)}, u32[]{:S(2)}, u32[]{:S(2)}) async-start(f32[32,96,2]{1,2,0:T(2,128)} %broadcast_in_dim.58), calls=%async_computation.7 | async-start | bytes 65536 | tf_op jit(solution)/shard_map/all_to_all | solution.py:30
  (2 other events, 1.3 us)
where the time goes:
time: 329 us; the launch traced here: 328 us
  waiting for transfers between devices  159 us (48%)
  starting transfers between devices  57.3 us (17%)
  blocking collectives  46 us (14%)
  local copies, waits for them, and re-layouts  37.1 us (11%)
  matrix products  18.8 us (6%)
  other arithmetic  8.29 us (3%)
    all_to_all x3, waiting for transfers between devices, copy_for_each(): lax.all_to_all(jnp.broadcast_to(x[None], (devices, *x.shape)), axis, 0, 0...  62.5 us
    all_to_all x2, waiting for transfers between devices, sum_at_owner(): pieces = lax.all_to_all(split_up(x, dim, devices), axis, 0, 0, tiled=True)  54.9 us
    all_to_all x1, blocking collectives, body(): lax.all_to_all(gate_grad, 'tp', split_axis=0, concat_axis=1, tiled=True)  29 us
    all_to_all x3, starting transfers between devices, copy_for_each(): lax.all_to_all(jnp.broadcast_to(x[None], (devices, *x.shape)), axis, 0, 0...  23.4 us
    all_to_all x1, waiting for transfers between devices, body(): lax.all_to_all(up_grad, 'tp', split_axis=0, concat_axis=1, tiled=True)  18.3 us
    all_to_all x1, blocking collectives, in_one_piece(): lax.all_to_all(both, axis, split_axis=split_dim, concat_axis=concat_dim,...  17 us
    all_to_all x1, waiting for transfers between devices, body(): lax.all_to_all(down_grad.astype(jnp.bfloat16), 'tp', split_axis=1, concat...  17 us
    all_to_all x2, starting transfers between devices, sum_at_owner(): pieces = lax.all_to_all(split_up(x, dim, devices), axis, 0, 0, tiled=True)  13.2 us
  transfers between devices with their start and end apart: 9, of which 8 were waited for; matrix products, arithmetic and copies ran while one was open for 13% of the time, Pallas kernels for 0%

commit v1 on v0

v1 whole, which is shorter than its diff:
```python
import jax
import jax.numpy as jnp
from jax import lax
from jax.experimental import pallas as pl
from jax.experimental.pallas import tpu as pltpu
from jax.sharding import PartitionSpec as P

BF = jnp.bfloat16
F32 = jnp.float32


def dot(a, b, ca, cb):
    return lax.dot_general(a, b, (((ca,), (cb,)), ((), ())), preferred_element_type=F32)


def halves(v):
    hi = v.astype(BF)
    return hi, (v - hi.astype(F32)).astype(BF)


def lay_out(pieces):
    n, rows, total = pieces.shape
    width = total // 3

    def kernel(src, *refs):
        outs, sems = refs[:3], refs[3]
        copies = []
        for m in range(3):
            for s in range(n):
                copies.append(
                    pltpu.make_async_copy(
                        src.at[s, :, pl.ds(m * width, width)],
                        outs[m].at[:, pl.ds(s * width, width)],
                        sems.at[m * n + s],
                    )
                )
        for c in copies:
            c.start()
        for c in copies:
            c.wait()

    return pl.pallas_call(
        kernel,
        out_shape=[jax.ShapeDtypeStruct((rows, n * width), pieces.dtype)] * 3,
        in_specs=[pl.BlockSpec(memory_space=pl.ANY)],
        out_specs=[pl.BlockSpec(memory_space=pl.ANY)] * 3,
        scratch_shapes=[pltpu.SemaphoreType.DMA((3 * n,))],
        name="lay_out",
    )(pieces)


def body(tokens, cotangent, expert_ids, combine_weights, w_gate, w_up, w_down):
    groups = lax.axis_size("ep")
    devices = lax.axis_size("tp")
    chips = devices // 2
    tok_rows, width = tokens.shape
    chosen = expert_ids.shape[1]
    cap = tok_rows * chosen * 5 // (3 * groups)
    rows = groups * cap
    wg, wu, wd = w_gate[0], w_up[0], w_down[0]
    hid = wg.shape[1]
    feats = wg.shape[0]
    core = lax.axis_index("tp") % 2
    same_core = [[2 * i + c for i in range(chips)] for c in range(2)]
    swap = [(i, i ^ 1) for i in range(devices)]

    ids = [expert_ids[:, k] for k in range(chosen)]
    hot = [
        (i[:, None] == jnp.arange(groups, dtype=jnp.int32)[None, :]).astype(F32) for i in ids
    ]
    both = sum(hot)
    t = jnp.arange(tok_rows, dtype=jnp.int32)
    before = jnp.dot((t[:, None] > t[None, :]).astype(F32), both)
    place = []
    for k in range(chosen):
        rank = jnp.sum(before * hot[k], axis=1).astype(jnp.int32)
        slot = ids[k] * cap + rank
        place.append((slot[None, :] == jnp.arange(rows, dtype=jnp.int32)[:, None]).astype(BF))
    cot = cotangent.astype(F32)
    weight = [combine_weights[:, k][:, None] for k in range(chosen)]
    send_rows = dot(sum(place), tokens, 1, 0)
    send_grad = sum(dot(place[k], (weight[k] * cot).astype(BF), 1, 0) for k in range(chosen))
    send = jnp.concatenate(
        [send_rows.reshape(groups, cap, width), send_grad.reshape(groups, cap, width)], axis=1
    ).astype(BF)
    recv = lax.all_to_all(send, "ep", 0, 0, tiled=True)
    piece = (
        jnp.concatenate(
            [recv[:, :cap].reshape(rows, width), recv[:, cap:].reshape(rows, width)], axis=0
        )
    ).T

    mine = lax.all_to_all(
        jnp.broadcast_to(piece[None], (chips, *piece.shape)),
        "tp", 0, 0, tiled=True, axis_index_groups=same_core,
    )
    theirs = lax.ppermute(mine, "tp", swap)
    full = jnp.where(
        (jnp.arange(2) == core)[None, :, None, None], mine[:, None], theirs[:, None]
    ).reshape(feats, 2 * rows)
    x, dy = full[:, :rows], full[:, rows:]

    gate_pre = dot(x, wg, 0, 0)
    up_pre = dot(x, wu, 0, 0)
    sigma = jax.nn.sigmoid(gate_pre)
    active = gate_pre * sigma
    slope = sigma * (1.0 + gate_pre * (1.0 - sigma))
    hidden = (active * up_pre).astype(BF)
    grad_hidden = dot(dy, wd, 0, 1)
    ggp = (grad_hidden * up_pre * slope).astype(BF)
    gup = (grad_hidden * active).astype(BF)
    inner = jnp.sum(hidden.astype(F32) * grad_hidden, axis=1)

    out_t = dot(wd, hidden, 0, 1)
    in_t = dot(wg, ggp, 1, 1) + dot(wu, gup, 1, 1)
    part = jnp.concatenate([out_t, in_t], axis=1).astype(BF).reshape(chips, 2, width, 2 * rows)
    keep = lax.dynamic_index_in_dim(part, core, 1, keepdims=False)
    give = lax.dynamic_index_in_dim(part, 1 - core, 1, keepdims=False)
    got = lax.ppermute(give, "tp", swap)
    inner = inner + lax.ppermute(inner, "tp", swap)
    hi, lo = halves(inner)
    extra = jnp.pad(jnp.stack([hi, lo]), ((0, 6), (0, rows)))
    reduced = (keep.astype(F32) + got.astype(F32)).astype(BF)
    reduced = jnp.concatenate(
        [reduced, jnp.broadcast_to(extra[None], (chips, 8, 2 * rows))], axis=1
    )
    summed = jnp.sum(
        lax.all_to_all(
            reduced, "tp", 0, 0, tiled=True, axis_index_groups=same_core
        ).astype(F32),
        axis=0,
    )

    both_grads = dot(x, jnp.concatenate([ggp, gup], axis=1), 1, 0).astype(BF)
    down_grad = dot(dy, hidden, 1, 0).astype(BF)
    grads = jnp.concatenate([both_grads, down_grad], axis=1).reshape(devices, width, 3 * hid)
    pieces = lax.all_to_all(grads, "tp", 0, 0, tiled=True)

    hi, lo = halves(summed[width] + summed[width + 1])
    back = jnp.concatenate(
        [summed[:width].astype(BF), hi[None], lo[None], jnp.zeros((6, 2 * rows), BF)], axis=0
    ).T.reshape(2, groups, cap, width + 8)
    back = jnp.concatenate([back[0], back[1]], axis=1)
    back = lax.all_to_all(back, "ep", 0, 0, tiled=True)
    out_back = back[:, :cap].reshape(rows, width + 8)
    in_back = back[:, cap:].reshape(rows, width + 8)
    chosen_out = [dot(place[k], out_back, 0, 0) for k in range(chosen)]
    mixed = sum(weight[k] * chosen_out[k][:, :width] for k in range(chosen)).astype(BF)
    grad_combine = jnp.concatenate(
        [
            (chosen_out[k][:, width : width + 1] + chosen_out[k][:, width + 1 : width + 2])
            / weight[k]
            for k in range(chosen)
        ],
        axis=1,
    )
    grad_tokens = dot(sum(place), in_back[:, :width], 0, 0).astype(BF)

    gate_out, up_out, down_out = lay_out(pieces)
    return (
        mixed,
        grad_tokens,
        grad_combine,
        gate_out[None],
        up_out[None],
        down_out.T[None],
    )


def solution(mesh):
    return jax.shard_map(
        body,
        mesh=mesh,
        in_specs=(
            P("ep", "tp"),
            P("ep", "tp"),
            P("ep", None),
            P("ep", None),
            P("ep", None, "tp"),
            P("ep", None, "tp"),
            P("ep", "tp", None),
        ),
        out_specs=(
            P("ep", "tp"),
            P("ep", "tp"),
            P("ep", None),
            P("ep", "tp", None),
            P("ep", "tp", None),
            P("ep", None, "tp"),
        ),
        check_vma=False,
    )
```

time: 329 us -> 359 us (1.091)
  Pallas kernels: 0 us -> 145 us
  waiting for transfers between devices: 159 us -> 87 us
  starting transfers between devices: 57.3 us -> 18.4 us
  local copies, waits for them, and re-layouts: 37.1 us -> 17.7 us
  other arithmetic: 8.29 us -> 20 us
    pallas_call x0 -> x1, Pallas kernels: none -> 145 us  [lay_out(): pl.pallas_call(kernel, out_shape=[jax.ShapeDtypeStruct((rows, n * width),...]
    all_to_all x9 -> x3, waiting for transfers between devices: 159 us -> 79.6 us  [the longest x1 52.9 us: body(): pieces = lax.all_to_all(grads, 'tp', 0, 0, tiled=True)]
    all_to_all x9 -> x3, starting transfers between devices: 57.3 us -> 14 us  [the longest x1 5.84 us: body(): pieces = lax.all_to_all(grads, 'tp', 0, 0, tiled=True)]
    broadcast_in_dim x10 -> x5, local copies, waits for them, and re-layouts: 14 us -> 0.34 us  [the longest x2 0.17 us: body(): jnp.where((jnp.arange(2) == core)[None, :, None, None], mine[:, None], th...]
    ppermute x0 -> x3, waiting for transfers between devices: none -> 7.36 us  [the longest x1 3.81 us: body(): inner = inner + lax.ppermute(inner, 'tp', swap)]
    concatenate x1 -> x5, other arithmetic: 0.04 us -> 7.28 us  [the longest x1 4.41 us: body(): jnp.concatenate([both_grads, down_grad], axis=1)]
    convert_element_type x5 -> x0, local copies, waits for them, and re-layouts: 6.7 us -> none  [the longest x1 2.45 us: body(): input_partial.astype(jnp.bfloat16)]
    concatenate x0 -> x2, local copies, waits for them, and re-layouts: none -> 6.7 us  [the longest x1 6.62 us: body(): jnp.concatenate([both_grads, down_grad], axis=1)]
  transfers between devices with their start and end apart: 9 -> 6, of which waited for: 8 -> 4; matrix products, arithmetic and copies ran while one was open for 13% -> 6% of each run, Pallas kernels for 0% -> 0%
where the time goes in v1:
time: 359 us; the launch traced here: 355 us
  Pallas kernels  145 us (40%)
  waiting for transfers between devices  87 us (24%)
  blocking collectives  47.8 us (13%)
  other arithmetic  20 us (6%)
  matrix products  18.5 us (5%)
  starting transfers between devices  18.4 us (5%)
  local copies, waits for them, and re-layouts  17.7 us (5%)
    pallas_call x1, Pallas kernels, lay_out(): pl.pallas_call(kernel, out_shape=[jax.ShapeDtypeStruct((rows, n * width),...  145 us
    all_to_all x1, waiting for transfers between devices, body(): pieces = lax.all_to_all(grads, 'tp', 0, 0, tiled=True)  52.9 us
    all_to_all x1, blocking collectives, body(): lax.all_to_all(jnp.broadcast_to(piece[None], (chips, *piece.shape)), 'tp'...  30.7 us
    all_to_all x1, waiting for transfers between devices, body(): lax.all_to_all(reduced, 'tp', 0, 0, tiled=True, axis_index_groups=same_core)  26.7 us
    dot_general x14, matrix products, dot(): lax.dot_general(a, b, (((ca,), (cb,)), ((), ())), preferred_element_type=...  18.4 us
    all_to_all x1, blocking collectives, body(): recv = lax.all_to_all(send, 'ep', 0, 0, tiled=True)  17 us
  transfers between devices with their start and end apart: 6, of which 4 were waited for; matrix products, arithmetic and copies ran while one was open for 6% of the time, Pallas kernels for 0%

profile of v1, /device:TPU:1, one launch (start us, length us, event | category | flops | bytes accessed | tf_op | source)
XLA Modules:
  0.0 355.4 jit_solution(4556632252224660107)
XLA Ops:
  7.0 17.0 %all_to_all.25 = bf16[8,80,96]{2,1,0:T(8,128)(2,1)S(1)} all-to-all(bf16[8,80,96]{2,1,0:T(8,128)(2,1)S(1)} %pad_maximum_fusion.2), channel_id=1, replica_groups=mesh['ep'=8,'tp'=32] {'ep'}, dimensions={0} | all-to-all | bytes 245760 | tf_op jit(solution)/shard_map/all_to_all | solution.py:86
  24.4 30.7 %all_to_all.26 = bf16[16,96,640]{2,1,0:T(8,128)(2,1)S(1)} all-to-all(bf16[16,96,640]{2,1,0:T(8,128)(2,1)S(1)} %broadcast_in_dim.72), channel_id=1, replica_groups={{0,2,4,6,8,10,12,14,16,18,20,22,24,26,28,30},{1,3,5,7,9,11,13,15,17,19,..., dimensions={0} | all-to-all | bytes 3932160 | tf_op jit(solution)/shard_map/all_to_all | solution.py:93
  55.1 3.9 %collective-permute-start = (bf16[16,96,640]{2,1,0:T(8,128)(2,1)S(1)}, bf16[16,96,640]{2,1,0:T(8,128)(2,1)}, u32[]{:S(2)}, u32[]{:S(2)}) collective-permute-start(bf16[16,96,640]{2,1,0:T(8,128)(2,1)S(1)} %all_to_all.26), channel_id=1, source_target_pairs={{0,1},{1,0},{2,3},{3,2},{4,5},{5,4},{6,7},{7,6},{8,9},{9,8},{10,11... | collective-permute-start | bytes 5898248 | tf_op jit(solution)/shard_map/ppermute | solution.py:97
  59.2 3.5 collective-permute-done
  62.7 2.2 bitcast_select_fusion
  65.8 1.8 copy-done.3
  68.3 2.3 multiply_reduce_fusion
  72.0 2.4 copy.31
  74.4 2.3 fusion.20
  77.5 2.5 copy.32
  80.0 3.6 %fusion.8 = bf16[16,96,640]{2,1,0:T(8,128)(2,1)} fusion(s32[]{:T(128)S(6)} %select_n.22, bf16[16,2,96,320]{3,2,1,0:T(8,128)(2,1)} %bitcast.71, bf16[16,2,96,320]{3,2,1,0:T(8,128)(2,1)} %bitcast.73), kind=kLoop, calls=%fused_computation.21 | loop fusion | flops 3932160 | bytes 5898244 | tf_op jit(solution)/shard_map/jit(dynamic_index_in_dim)/squeeze | solution.py:118
  84.1 3.8 %collective-permute-done.2 = f32[320]{0:T(512)} collective-permute-done((f32[320]{0:T(512)S(1)}, f32[320]{0:T(512)}, u32[]{:S(2)}, u32[]{:S(2)}) %collective-permute-start.2) | collective-permute-done | bytes 1312 | tf_op jit(solution)/shard_map/ppermute | solution.py:120
  88.6 2.6 fusion.1
  92.7 4.7 %all-to-all-start.2 = ((bf16[16,104,640]{2,1,0:T(8,128)(2,1)}), bf16[16,104,640]{2,1,0:T(8,128)(2,1)}, u32[]{:S(2)}, u32[]{:S(2)}) async-start(bf16[16,104,640]{2,1,0:T(8,128)(2,1)} %pad_maximum_fusion.1), calls=%async_computation.2 | async-start | bytes 4259840 | tf_op jit(solution)/shard_map/all_to_all | solution.py:128
  97.6 3.0 convolution_convert_fusion.2
  100.6 3.5 convolution_convert_fusion
  104.1 26.7 %all-to-all-done.2 = bf16[16,104,640]{2,1,0:T(8,128)(2,1)} async-done(((bf16[16,104,640]{2,1,0:T(8,128)(2,1)}), bf16[16,104,640]{2,1,0:T(8,128)(2,1)}, u32[]{:S(2)}, u32[]{:S(2)}) %all-to-all-start.2) | async-done | bytes 2129952 | tf_op jit(solution)/shard_map/all_to_all | solution.py:128
  130.8 1.9 convert_reduce_fusion
  133.9 3.4 all-to-all-start.3
  137.3 4.4 %pad_maximum_fusion = bf16[3072,768]{0,1:T(8,128)(2,1)} fusion(bf16[3072,256]{0,1:T(8,128)(2,1)S(1)} %convolution_convert_fusion.2, bf16[3072,512]{0,1:T(8,128)(2,1)} %convolution_convert_fusion), kind=kLoop, calls=%fused_computation | loop fusion | flops 9437184 | bytes 9437184 | tf_op jit(solution)/shard_map/concatenate | solution.py:136
  141.7 6.6 %copy.37 = bf16[3072,768]{1,0:T(8,128)(2,1)} copy(bf16[3072,768]{0,1:T(8,128)(2,1)} %pad_maximum_fusion) | data formatting | bytes 9437184 | tf_op jit(solution)/shard_map/concatenate | solution.py:136
  148.4 5.8 %all-to-all-start.4 = ((bf16[32,96,768]{2,1,0:T(8,128)(2,1)}), bf16[32,96,768]{2,1,0:T(8,128)(2,1)}, u32[]{:S(2)}, u32[]{:S(2)}) async-start(bf16[32,96,768]{2,1,0:T(8,128)(2,1)} %bitcast.75), calls=%async_computation.4 | async-start | bytes 9437184 | tf_op jit(solution)/shard_map/all_to_all | solution.py:137
  157.4 52.9 %all-to-all-done.4.src = bf16[32,96,768]{2,1,0:T(8,128)(2,1)} async-done(((bf16[32,96,768]{2,1,0:T(8,128)(2,1)}), bf16[32,96,768]{2,1,0:T(8,128)(2,1)}, u32[]{:S(2)}, u32[]{:S(2)}) %all-to-all-start.4) | async-done | bytes 4718624 | tf_op jit(solution)/shard_map/all_to_all | solution.py:137
  210.4 144.9 %lay_out.1 = (bf16[96,8192]{1,0:T(8,128)(2,1)}, bf16[96,8192]{1,0:T(8,128)(2,1)}, bf16[96,8192]{1,0:T(8,128)(2,1)}) custom-call(bf16[32,96,768]{2,1,0:T(8,128)(2,1)} %all-to-all-done.4.src), custom_call_target="tpu_custom_call" | custom-call | tf_op jit(solution)/shard_map/lay_out/pallas_call | solution.py:42
  (89 shorter events, 17.7 us)
Async XLA Ops:
  0.6 67.7 %copy-start = (bf16[1,256,3072]{2,1,0:T(8,128)(2,1)S(1)}, bf16[1,256,3072]{2,1,0:T(8,128)(2,1)}, u32[]{:S(2)}) copy-start(bf16[1,256,3072]{2,1,0:T(8,128)(2,1)} %param.13) | copy-start | bytes 4718596
  2.7 3.1 copy-start.11
  3.7 2.2 copy-start.13
  3.7 20.4 %copy-start.15 = (s32[96]{0:T(128)}, s32[96]{0:T(128)S(1)}, u32[]{:S(2)}) copy-start(s32[96]{0:T(128)S(1)} %get-tuple-element.45) | copy-start | bytes 1156
  55.1 7.6 %collective-permute-start = (bf16[16,96,640]{2,1,0:T(8,128)(2,1)S(1)}, bf16[16,96,640]{2,1,0:T(8,128)(2,1)}, u32[]{:S(2)}, u32[]{:S(2)}) collective-permute-start(bf16[16,96,640]{2,1,0:T(8,128)(2,1)S(1)} %all_to_all.26), channel_id=1, source_target_pairs={{0,1},{1,0},{2,3},{3,2},{4,5},{5,4},{6,7},{7,6},{8,9},{9,8},{10,11... | collective-permute-start | bytes 5898248 | tf_op jit(solution)/shard_map/ppermute | solution.py:97
  59.2 5.7 %copy-start.4 = (bf16[1,3072,256]{2,1,0:T(8,128)(2,1)S(1)}, bf16[1,3072,256]{2,1,0:T(8,128)(2,1)}, u32[]{:S(2)}) copy-start(bf16[1,3072,256]{2,1,0:T(8,128)(2,1)} %param.12) | copy-start | bytes 4718596
  64.9 3.4 copy-start.1
  64.9 2.6 copy-start.3
  74.4 2.3 copy-start.5
  74.4 2.3 copy-start.9
  83.6 5.0 %collective-permute-start.1 = (bf16[16,96,640]{2,1,0:T(8,128)(2,1)}, bf16[16,96,640]{2,1,0:T(8,128)(2,1)S(1)}, u32[]{:S(2)}, u32[]{:S(2)}) collective-permute-start(bf16[16,96,640]{2,1,0:T(8,128)(2,1)} %fusion.8), channel_id=1, source_target_pairs={{0,1},{1,0},{2,3},{3,2},{4,5},{5,4},{6,7},{7,6},{8,9},{9,8},{10,11... | collective-permute-start | bytes 5898248 | tf_op jit(solution)/shard_map/ppermute | solution.py:119
  83.9 3.9 %collective-permute-start.2 = (f32[320]{0:T(512)S(1)}, f32[320]{0:T(512)}, u32[]{:S(2)}, u32[]{:S(2)}) collective-permute-start(f32[320]{0:T(512)S(1)} %get-tuple-element.26), channel_id=1, source_target_pairs={{0,1},{1,0},{2,3},{3,2},{4,5},{5,4},{6,7},{7,6},{8,9},{9,8},{10,11... | collective-permute-start | bytes 3848 | tf_op jit(solution)/shard_map/ppermute | solution.py:120
  92.7 4.9 %copy-start.8 = (bf16[320,256]{1,0:T(8,128)(2,1)S(1)}, bf16[320,256]{1,0:T(8,128)(2,1)}, u32[]{:S(2)}) copy-start(bf16[320,256]{1,0:T(8,128)(2,1)} %copy-done.7) | copy-start | bytes 491524
  92.7 7.9 %copy-start.10 = (bf16[320,256]{1,0:T(8,128)(2,1)S(1)}, bf16[320,256]{1,0:T(8,128)(2,1)}, u32[]{:S(2)}) copy-start(bf16[320,256]{1,0:T(8,128)(2,1)} %get-tuple-element.29) | copy-start | bytes 491524
  92.7 38.1 %all-to-all-start.2 = ((bf16[16,104,640]{2,1,0:T(8,128)(2,1)}), bf16[16,104,640]{2,1,0:T(8,128)(2,1)}, u32[]{:S(2)}, u32[]{:S(2)}) async-start(bf16[16,104,640]{2,1,0:T(8,128)(2,1)} %pad_maximum_fusion.1), calls=%async_computation.2 | async-start | bytes 4259840 | tf_op jit(solution)/shard_map/all_to_all | solution.py:128
  97.5 3.1 copy-start.2
  97.5 3.1 copy-start.6
  133.9 14.4 %all-to-all-start.3 = ((bf16[8,80,104]{2,1,0:T(8,128)(2,1)}), bf16[8,80,104]{2,1,0:T(8,128)(2,1)S(1)}, u32[]{:S(2)}, u32[]{:S(2)}) async-start(bf16[8,80,104]{2,1,0:T(8,128)(2,1)} %pad_maximum_fusion.3), calls=%async_computation.3 | async-start | bytes 327680 | tf_op jit(solution)/shard_map/all_to_all | solution.py:144
  148.3 5.9 %copy-start.18 = (f32[96,1]{0,1:T(1,128)S(1)}, f32[96,1]{0,1:T(1,128)}, u32[]{:S(2)}) copy-start(f32[96,1]{0,1:T(1,128)} %get-tuple-element.43) | copy-start | bytes 1156
  148.3 6.0 %copy-start.17 = (f32[96,1]{0,1:T(1,128)S(1)}, f32[96,1]{0,1:T(1,128)}, u32[]{:S(2)}) copy-start(f32[96,1]{0,1:T(1,128)} %get-tuple-element.40) | copy-start | bytes 1156
  148.3 6.1 %copy-start.14 = (s32[96]{0:T(128)S(1)}, s32[96]{0:T(128)}, u32[]{:S(2)}) copy-start(s32[96]{0:T(128)} %copy-done.13) | copy-start | bytes 1156
  148.4 6.5 %copy-start.16 = (s32[96]{0:T(128)S(1)}, s32[96]{0:T(128)}, u32[]{:S(2)}) copy-start(s32[96]{0:T(128)} %copy-done.15) | copy-start | bytes 1156
  148.4 8.4 %copy-start.12 = (f32[96]{0:T(128)S(1)}, f32[96]{0:T(128)}, u32[]{:S(2)}) copy-start(f32[96]{0:T(128)} %copy-done.11) | copy-start | bytes 1156
  148.4 62.0 %all-to-all-start.4 = ((bf16[32,96,768]{2,1,0:T(8,128)(2,1)}), bf16[32,96,768]{2,1,0:T(8,128)(2,1)}, u32[]{:S(2)}, u32[]{:S(2)}) async-start(bf16[32,96,768]{2,1,0:T(8,128)(2,1)} %bitcast.75), calls=%async_computation.4 | async-start | bytes 9437184 | tf_op jit(solution)/shard_map/all_to_all | solution.py:137
  (1 other events, 0.7 us)
